TPU v7x, 256 devices: a whole 4x4x8 slice. The times are simulated.
256 devices in a mesh: trial: 2 (over core), qa: 16 (over y, x), qb: 8 (over z).
Axes of the slice: x: 4, y: 4, z: 8, core: 2. Of those that a mesh axis runs over, the one named last changes fastest.
Arguments:
- wave_parts: float32 [4, 512, 128, 128], P('trial', ('qa', 'qb')), parts along dimension 0, may hold values from -6 to 6
- level_table: float32 [1024, 128, 128], P(('trial', 'qa', 'qb')), parts along dimension 0, may hold values from -2 to 2
- diagonal_angles: float32 [6, 128], P('trial'), parts along dimension 0, may hold values from 0.3 to 1.2
- turn_angles: float32 [6, 4], P('trial'), parts along dimension 0, may hold values from 0.3 to 1.2
Outputs:
- final_parts: float32 [4, 512, 128, 128], P('trial', ('qa', 'qb')), parts along dimension 0
There are 2 independent parts, one for each index of `trial`. A program takes and returns all parts, laid end to end along the dimension named above; each array names one. Nothing has to cross between parts.
All inputs are finite; a program needn't handle non-finite values.
Results may differ from a plain program's by a relative error of at most 0.0003.
Values sent between devices are 32-bit elements.
A program may use at most 64 MiB of HBM per device.

v0:
```python
import jax
import jax.numpy as jnp
from jax import lax
from jax.sharding import PartitionSpec as P

LAYERS = 3


def count_bits(values, count):
    places = jnp.arange(count.bit_length() - 1, dtype=jnp.int32)
    return jnp.sum(values[..., None] >> places & 1, axis=-1)


def rotation_table(count, angle):
    rank = jnp.arange(count, dtype=jnp.int32)
    apart = count_bits(rank[:, None] ^ rank[None, :], count)
    bits = count.bit_length() - 1
    size = jnp.cos(angle) ** (bits - apart).astype(jnp.float32) * jnp.sin(angle) ** apart.astype(
        jnp.float32
    )
    real_sign = jnp.where(apart % 4 == 0, 1.0, jnp.where(apart % 4 == 2, -1.0, 0.0)).astype(
        jnp.float32
    )
    imag_sign = jnp.where(apart % 4 == 1, -1.0, jnp.where(apart % 4 == 3, 1.0, 0.0)).astype(
        jnp.float32
    )
    return (size * real_sign, size * imag_sign)


def mix_dim(values, dim, angle):
    real_part, imag_part = rotation_table(values.shape[dim], angle)

    def times(table):
        moved = jnp.tensordot(values, table, axes=([dim], [0]), precision=lax.Precision.HIGHEST)
        return jnp.moveaxis(moved, -1, dim)

    by_real = times(real_part)
    by_imag = times(imag_part)
    return jnp.stack([by_real[0] - by_imag[1], by_real[1] + by_imag[0]])


def phase_step(values, levels, angle):
    turn = angle * levels
    return jnp.stack(
        [
            values[0] * jnp.cos(turn) + values[1] * jnp.sin(turn),
            values[1] * jnp.cos(turn) - values[0] * jnp.sin(turn),
        ]
    )


def shards(wave_parts, level_table, diagonal_angles, turn_angles):
    values = wave_parts
    for layer in range(LAYERS):
        values = phase_step(values, level_table, diagonal_angles[layer])
        values = mix_dim(values, 3, turn_angles[layer, 0])
        values = mix_dim(values, 2, turn_angles[layer, 1])
        moved = lax.all_to_all(values, "qa", split_axis=2, concat_axis=1, tiled=True)
        moved = mix_dim(moved, 1, turn_angles[layer, 2])
        values = lax.all_to_all(moved, "qa", split_axis=1, concat_axis=2, tiled=True)
        moved = lax.all_to_all(values, "qb", split_axis=3, concat_axis=1, tiled=True)
        spread = moved.reshape(2, lax.axis_size("qb"), -1, moved.shape[2], moved.shape[3])
        moved = mix_dim(spread, 1, turn_angles[layer, 3]).reshape(moved.shape)
        values = lax.all_to_all(moved, "qb", split_axis=1, concat_axis=3, tiled=True)
    return values


def solution(mesh):
    placed = (
        P("trial", ("qa", "qb"), None, None),
        P(("trial", "qa", "qb"), None, None),
        P("trial", None),
        P("trial", None),
    )
    return jax.shard_map(
        shards,
        mesh=mesh,
        in_specs=placed,
        out_specs=P("trial", ("qa", "qb"), None, None),
        check_vma=False,
    )
```

profile of v0, /device:TPU:2, one launch (start us, length us, event | category | flops | bytes accessed | tf_op | source)
XLA Modules:
  0.0 244.2 jit_solution(5712961371041318198)
XLA Ops:
  0.0 1.8 fusion.327
  3.8 2.0 fusion.19
  9.0 1.1 convolution_bitcast_fusion.17
  10.1 1.1 convolution_bitcast_fusion.16
  11.3 1.0 copy.169
  12.3 7.5 %all-to-all-start = ((f32[2,4,128,128]{3,1,0,2:T(4,128)}), f32[2,4,128,128]{3,1,0,2:T(4,128)S(1)}, u32[]{:S(2)}, u32[]{:S(2)}) async-start(f32[2,4,128,128]{3,1,0,2:T(4,128)} %copy.169), calls=%async_computation | async-start | bytes 1048576 | tf_op jit(solution)/shard_map/all_to_all | solution.py:58
  21.3 9.2 %all-to-all-done = f32[2,4,128,128]{3,1,0,2:T(4,128)S(1)} async-done(((f32[2,4,128,128]{3,1,0,2:T(4,128)}), f32[2,4,128,128]{3,1,0,2:T(4,128)S(1)}, u32[]{:S(2)}, u32[]{:S(2)}) %all-to-all-start) | async-done | bytes 524320 | tf_op jit(solution)/shard_map/all_to_all | solution.py:58
  32.9 13.5 %all_to_all.201 = f32[2,64,8,128]{3,2,0,1:T(8,128)S(1)} all-to-all(f32[2,64,8,128]{3,2,0,1:T(8,128)S(1)} %copy.174), channel_id=1, replica_groups=mesh['trial'=2,'qa'=16,'qb'=8] {'qa'}, dimensions={1} | all-to-all | bytes 1048576 | tf_op jit(solution)/shard_map/all_to_all | solution.py:60
  46.4 1.0 copy.177
  47.4 8.5 %all-to-all-start.2 = ((f32[2,4,128,128]{2,1,0,3:T(4,128)}), f32[2,4,128,128]{2,1,0,3:T(4,128)S(1)}, u32[]{:S(2)}, u32[]{:S(2)}) async-start(f32[2,4,128,128]{2,1,0,3:T(4,128)} %copy.177), calls=%async_computation.2 | async-start | bytes 1048576 | tf_op jit(solution)/shard_map/all_to_all | solution.py:61
  57.4 14.1 %all-to-all-done.2 = f32[2,4,128,128]{2,1,0,3:T(4,128)S(1)} async-done(((f32[2,4,128,128]{2,1,0,3:T(4,128)}), f32[2,4,128,128]{2,1,0,3:T(4,128)S(1)}, u32[]{:S(2)}, u32[]{:S(2)}) %all-to-all-start.2) | async-done | bytes 524320 | tf_op jit(solution)/shard_map/all_to_all | solution.py:61
  74.4 3.7 %all-to-all-start.3 = ((f32[2,32,128,16]{2,3,0,1:T(8,128)}), f32[2,32,128,16]{2,3,0,1:T(8,128)S(1)}, u32[]{:S(2)}, u32[]{:S(2)}) async-start(f32[2,32,128,16]{2,3,0,1:T(8,128)} %copy.184), calls=%async_computation.3 | async-start | bytes 1048576 | tf_op jit(solution)/shard_map/all_to_all | solution.py:64
  80.7 10.9 %all-to-all-done.3 = f32[2,32,128,16]{2,3,0,1:T(8,128)S(1)} async-done(((f32[2,32,128,16]{2,3,0,1:T(8,128)}), f32[2,32,128,16]{2,3,0,1:T(8,128)S(1)}, u32[]{:S(2)}, u32[]{:S(2)}) %all-to-all-start.3) | async-done | bytes 524320 | tf_op jit(solution)/shard_map/all_to_all | solution.py:64
  92.8 1.0 add_bitcast_fusion.1
  95.4 1.1 convolution_bitcast_fusion.11
  96.5 1.1 convolution_bitcast_fusion.10
  98.7 7.6 %all-to-all-start.4 = ((f32[2,4,128,128]{3,1,0,2:T(4,128)}), f32[2,4,128,128]{3,1,0,2:T(4,128)S(1)}, u32[]{:S(2)}, u32[]{:S(2)}) async-start(f32[2,4,128,128]{3,1,0,2:T(4,128)} %copy.194), calls=%async_computation.4 | async-start | bytes 1048576 | tf_op jit(solution)/shard_map/all_to_all | solution.py:58
  107.7 7.3 %all-to-all-done.4 = f32[2,4,128,128]{3,1,0,2:T(4,128)S(1)} async-done(((f32[2,4,128,128]{3,1,0,2:T(4,128)}), f32[2,4,128,128]{3,1,0,2:T(4,128)S(1)}, u32[]{:S(2)}, u32[]{:S(2)}) %all-to-all-start.4) | async-done | bytes 524320 | tf_op jit(solution)/shard_map/all_to_all | solution.py:58
  117.4 12.7 %all_to_all.202 = f32[2,64,8,128]{3,2,0,1:T(8,128)S(1)} all-to-all(f32[2,64,8,128]{3,2,0,1:T(8,128)S(1)} %copy.199), channel_id=1, replica_groups=mesh['trial'=2,'qa'=16,'qb'=8] {'qa'}, dimensions={1} | all-to-all | bytes 1048576 | tf_op jit(solution)/shard_map/all_to_all | solution.py:60
  131.2 3.5 %all-to-all-start.6 = ((f32[2,4,128,128]{2,1,0,3:T(4,128)}), f32[2,4,128,128]{2,1,0,3:T(4,128)S(1)}, u32[]{:S(2)}, u32[]{:S(2)}) async-start(f32[2,4,128,128]{2,1,0,3:T(4,128)} %copy.202), calls=%async_computation.6 | async-start | bytes 1048576 | tf_op jit(solution)/shard_map/all_to_all | solution.py:61
  136.0 14.0 %all-to-all-done.6 = f32[2,4,128,128]{2,1,0,3:T(4,128)S(1)} async-done(((f32[2,4,128,128]{2,1,0,3:T(4,128)}), f32[2,4,128,128]{2,1,0,3:T(4,128)S(1)}, u32[]{:S(2)}, u32[]{:S(2)}) %all-to-all-start.6) | async-done | bytes 524320 | tf_op jit(solution)/shard_map/all_to_all | solution.py:61
  152.9 3.7 %all-to-all-start.7 = ((f32[2,32,128,16]{2,3,0,1:T(8,128)}), f32[2,32,128,16]{2,3,0,1:T(8,128)S(1)}, u32[]{:S(2)}, u32[]{:S(2)}) async-start(f32[2,32,128,16]{2,3,0,1:T(8,128)} %copy.209), calls=%async_computation.7 | async-start | bytes 1048576 | tf_op jit(solution)/shard_map/all_to_all | solution.py:64
  159.5 12.0 %all-to-all-done.7 = f32[2,32,128,16]{2,3,0,1:T(8,128)S(1)} async-done(((f32[2,32,128,16]{2,3,0,1:T(8,128)}), f32[2,32,128,16]{2,3,0,1:T(8,128)S(1)}, u32[]{:S(2)}, u32[]{:S(2)}) %all-to-all-start.7) | async-done | bytes 524320 | tf_op jit(solution)/shard_map/all_to_all | solution.py:64
  171.9 1.0 add_bitcast_fusion
  174.6 1.1 convolution_bitcast_fusion.5
  175.7 1.1 convolution_bitcast_fusion.4
  177.9 5.8 %all-to-all-start.8 = ((f32[2,4,128,128]{3,1,0,2:T(4,128)}), f32[2,4,128,128]{3,1,0,2:T(4,128)S(1)}, u32[]{:S(2)}, u32[]{:S(2)}) async-start(f32[2,4,128,128]{3,1,0,2:T(4,128)} %copy.219), calls=%async_computation.8 | async-start | bytes 1048576 | tf_op jit(solution)/shard_map/all_to_all | solution.py:58
  185.1 7.3 %all-to-all-done.8 = f32[2,4,128,128]{3,1,0,2:T(4,128)S(1)} async-done(((f32[2,4,128,128]{3,1,0,2:T(4,128)}), f32[2,4,128,128]{3,1,0,2:T(4,128)S(1)}, u32[]{:S(2)}, u32[]{:S(2)}) %all-to-all-start.8) | async-done | bytes 524320 | tf_op jit(solution)/shard_map/all_to_all | solution.py:58
  194.7 12.7 %all_to_all.203 = f32[2,64,8,128]{3,2,0,1:T(8,128)S(1)} all-to-all(f32[2,64,8,128]{3,2,0,1:T(8,128)S(1)} %copy.224), channel_id=1, replica_groups=mesh['trial'=2,'qa'=16,'qb'=8] {'qa'}, dimensions={1} | all-to-all | bytes 1048576 | tf_op jit(solution)/shard_map/all_to_all | solution.py:60
  208.5 3.5 %all-to-all-start.10 = ((f32[2,4,128,128]{2,1,0,3:T(4,128)}), f32[2,4,128,128]{2,1,0,3:T(4,128)S(1)}, u32[]{:S(2)}, u32[]{:S(2)}) async-start(f32[2,4,128,128]{2,1,0,3:T(4,128)} %copy.227), calls=%async_computation.10 | async-start | bytes 1048576 | tf_op jit(solution)/shard_map/all_to_all | solution.py:61
  213.5 12.2 %all-to-all-done.10 = f32[2,4,128,128]{2,1,0,3:T(4,128)S(1)} async-done(((f32[2,4,128,128]{2,1,0,3:T(4,128)}), f32[2,4,128,128]{2,1,0,3:T(4,128)S(1)}, u32[]{:S(2)}, u32[]{:S(2)}) %all-to-all-start.10) | async-done | bytes 524320 | tf_op jit(solution)/shard_map/all_to_all | solution.py:61
  227.8 15.4 %all_to_all.204 = f32[2,32,128,16]{2,3,0,1:T(8,128)S(1)} all-to-all(f32[2,32,128,16]{2,3,0,1:T(8,128)S(1)} %copy.234), channel_id=1, replica_groups=mesh['trial'=2,'qa'=16,'qb'=8] {'qb'}, dimensions={1} | all-to-all | bytes 1048576 | tf_op jit(solution)/shard_map/all_to_all | solution.py:64
  (89 shorter events, 27.1 us)
Async XLA Ops:
  3.1 0.7 copy-start.1
  12.3 18.2 %all-to-all-start = ((f32[2,4,128,128]{3,1,0,2:T(4,128)}), f32[2,4,128,128]{3,1,0,2:T(4,128)S(1)}, u32[]{:S(2)}, u32[]{:S(2)}) async-start(f32[2,4,128,128]{3,1,0,2:T(4,128)} %copy.169), calls=%async_computation | async-start | bytes 1048576 | tf_op jit(solution)/shard_map/all_to_all | solution.py:58
  47.4 24.1 %all-to-all-start.2 = ((f32[2,4,128,128]{2,1,0,3:T(4,128)}), f32[2,4,128,128]{2,1,0,3:T(4,128)S(1)}, u32[]{:S(2)}, u32[]{:S(2)}) async-start(f32[2,4,128,128]{2,1,0,3:T(4,128)} %copy.177), calls=%async_computation.2 | async-start | bytes 1048576 | tf_op jit(solution)/shard_map/all_to_all | solution.py:61
  74.4 17.2 %all-to-all-start.3 = ((f32[2,32,128,16]{2,3,0,1:T(8,128)}), f32[2,32,128,16]{2,3,0,1:T(8,128)S(1)}, u32[]{:S(2)}, u32[]{:S(2)}) async-start(f32[2,32,128,16]{2,3,0,1:T(8,128)} %copy.184), calls=%async_computation.3 | async-start | bytes 1048576 | tf_op jit(solution)/shard_map/all_to_all | solution.py:64
  91.8 1.0 copy-start
  98.7 16.3 %all-to-all-start.4 = ((f32[2,4,128,128]{3,1,0,2:T(4,128)}), f32[2,4,128,128]{3,1,0,2:T(4,128)S(1)}, u32[]{:S(2)}, u32[]{:S(2)}) async-start(f32[2,4,128,128]{3,1,0,2:T(4,128)} %copy.194), calls=%async_computation.4 | async-start | bytes 1048576 | tf_op jit(solution)/shard_map/all_to_all | solution.py:58
  131.2 18.8 %all-to-all-start.6 = ((f32[2,4,128,128]{2,1,0,3:T(4,128)}), f32[2,4,128,128]{2,1,0,3:T(4,128)S(1)}, u32[]{:S(2)}, u32[]{:S(2)}) async-start(f32[2,4,128,128]{2,1,0,3:T(4,128)} %copy.202), calls=%async_computation.6 | async-start | bytes 1048576 | tf_op jit(solution)/shard_map/all_to_all | solution.py:61
  152.9 18.6 %all-to-all-start.7 = ((f32[2,32,128,16]{2,3,0,1:T(8,128)}), f32[2,32,128,16]{2,3,0,1:T(8,128)S(1)}, u32[]{:S(2)}, u32[]{:S(2)}) async-start(f32[2,32,128,16]{2,3,0,1:T(8,128)} %copy.209), calls=%async_computation.7 | async-start | bytes 1048576 | tf_op jit(solution)/shard_map/all_to_all | solution.py:64
  177.9 14.5 %all-to-all-start.8 = ((f32[2,4,128,128]{3,1,0,2:T(4,128)}), f32[2,4,128,128]{3,1,0,2:T(4,128)S(1)}, u32[]{:S(2)}, u32[]{:S(2)}) async-start(f32[2,4,128,128]{3,1,0,2:T(4,128)} %copy.219), calls=%async_computation.8 | async-start | bytes 1048576 | tf_op jit(solution)/shard_map/all_to_all | solution.py:58
  208.5 17.2 %all-to-all-start.10 = ((f32[2,4,128,128]{2,1,0,3:T(4,128)}), f32[2,4,128,128]{2,1,0,3:T(4,128)S(1)}, u32[]{:S(2)}, u32[]{:S(2)}) async-start(f32[2,4,128,128]{2,1,0,3:T(4,128)} %copy.227), calls=%async_computation.10 | async-start | bytes 1048576 | tf_op jit(solution)/shard_map/all_to_all | solution.py:61
where the time goes:
time: 246 us; the launch traced here: 244 us
  waiting for transfers between devices  87 us (35%)
  blocking collectives  54.3 us (22%)
  starting transfers between devices  43.6 us (18%)
  matrix products  20.9 us (8%)
  between operations  17.6 us (7%)
  local copies, waits for them, and re-layouts  15.4 us (6%)
  other arithmetic  5.26 us (2%)
    all_to_all x3, waiting for transfers between devices, shards(): lax.all_to_all(values, 'qb', split_axis=3, concat_axis=1, tiled=True)  40.4 us
    all_to_all x3, blocking collectives, shards(): lax.all_to_all(moved, 'qa', split_axis=1, concat_axis=2, tiled=True)  39 us
    all_to_all x3, waiting for transfers between devices, shards(): lax.all_to_all(values, 'qa', split_axis=2, concat_axis=1, tiled=True)  23.8 us
    all_to_all x2, waiting for transfers between devices, shards(): lax.all_to_all(moved, 'qb', split_axis=1, concat_axis=3, tiled=True)  22.8 us
    dot_general x24, matrix products, times(): jnp.tensordot(values, table, axes=([dim], [0]), precision=lax.Precision.H...  20.9 us
    all_to_all x3, starting transfers between devices, shards(): lax.all_to_all(values, 'qa', split_axis=2, concat_axis=1, tiled=True)  20.8 us
    all_to_all x3, starting transfers between devices, shards(): lax.all_to_all(values, 'qb', split_axis=3, concat_axis=1, tiled=True)  15.5 us
    all_to_all x1, blocking collectives, shards(): lax.all_to_all(moved, 'qb', split_axis=1, concat_axis=3, tiled=True)  15.4 us
  transfers between devices with their start and end apart: 8, of which 8 were waited for; matrix products, arithmetic and copies ran while one was open for 0% of the time, Pallas kernels for 0%

commit v1 on v0

v1 whole, which is shorter than its diff:
```python
import functools

import jax
import jax.numpy as jnp
from jax import lax
from jax.experimental import pallas as pl
from jax.experimental.pallas import tpu as pltpu
from jax.sharding import PartitionSpec as P

MESH = pl.DeviceIdType.MESH
F32 = jnp.float32
BF16 = jnp.bfloat16
PAD = 8


def split(x):
    high = x.astype(BF16)
    return high, (x - high.astype(F32)).astype(BF16)


def dot3(a, b, dims=((1,), (0,))):
    def one(x, y):
        return lax.dot_general(x, y, (dims, ((), ())), preferred_element_type=F32)

    (ah, al), (bh, bl) = a, b
    return one(ah, bh) + (one(ah, bl) + one(al, bh))


def sincos(x):
    turns = jnp.floor(x * 0.6366197723675814 + 0.5)
    y = (x - turns * 1.5707855224609375) - turns * 1.0804334124e-05
    z = y * y
    s = y + y * z * (-1.6666654611e-1 + z * (8.3321608736e-3 + z * -1.9515295891e-4))
    c = 1.0 - 0.5 * z + z * z * (4.166664568298827e-2 + z * (-1.388731625493765e-3 + z * 2.443315711809948e-5))
    quarter = turns - 4.0 * jnp.floor(turns * 0.25)
    odd = (quarter == 1.0) | (quarter == 3.0)
    sin = jnp.where(odd, c, s)
    cos = jnp.where(odd, s, c)
    sin = jnp.where(quarter >= 2.0, -sin, sin)
    cos = jnp.where((quarter == 1.0) | (quarter == 2.0), -cos, cos)
    return sin, cos


def phased(xr, xi, turn):
    s, c = sincos(turn)
    return xr * c + xi * s, xi * c - xr * s


def rotation(count, pairs):
    apart = lax.broadcasted_iota(jnp.int32, (count, count), 0) ^ lax.broadcasted_iota(jnp.int32, (count, count), 1)
    size = None
    ones = None
    for place, (c, s) in enumerate(pairs):
        bit = (apart >> place) & 1
        factor = jnp.where(bit == 1, s, c)
        size = factor if size is None else size * factor
        ones = bit if ones is None else ones + bit
    ones = ones & 3
    real = jnp.where(ones == 0, size, jnp.where(ones == 2, -size, 0.0))
    imag = jnp.where(ones == 1, -size, jnp.where(ones == 3, size, 0.0))
    return real, imag


def mix_blocks(parts, c, s):
    step = 1
    while step < len(parts):
        mixed = list(parts)
        for k in range(len(parts)):
            if not k & step:
                (ur, ui), (vr, vi) = parts[k], parts[k | step]
                mixed[k] = (c * ur + s * vi, c * ui - s * vr)
                mixed[k | step] = (c * vr + s * ui, c * vi - s * ur)
        parts = mixed
        step *= 2
    return parts


def body(
    nqa,
    nqb,
    wave,
    levels,
    diag,
    turns,
    out,
    mats,
    send1,
    send2,
    send3,
    land1,
    land2,
    land3,
    flip,
    tab2,
    tab3,
    work,
    ssem,
    rsem,
    tsend,
    trecv,
):
    n = nqa * nqb
    blocks = wave.shape[1]
    qa = lax.axis_index("qa")
    qb = lax.axis_index("qb")
    me = qa * nqb + qb
    near = list(range(1, nqb))
    near.sort(key=lambda d: -min(d, nqb - d))

    def peers(visit):
        @pl.loop(1, nqa)
        def _(da):
            for dz in near + [0]:
                visit(lax.rem(qa + da, nqa), lax.rem(qb + dz, nqb))

        for dz in near:
            visit(qa, lax.rem(qb + dz, nqb))

    bar = pltpu.get_barrier_semaphore()
    peers(lambda a, z: pl.semaphore_signal(bar, inc=1, device_id={"qa": a, "qb": z}, device_id_type=MESH))

    def spread(src, dst, ssem, rsem):
        def visit(a, z):
            pltpu.make_async_remote_copy(
                src_ref=src.at[:, pl.ds(a * nqb + z, 1), :],
                dst_ref=dst.at[:, pl.ds(me, 1), :],
                send_sem=ssem,
                recv_sem=rsem,
                device_id={"qa": a, "qb": z},
                device_id_type=MESH,
            ).start()

        peers(visit)
        pltpu.make_async_remote_copy(
            src_ref=src.at[:, pl.ds(0, 1), :],
            dst_ref=dst.at[:, pl.ds(n, 1), :],
            send_sem=ssem,
            recv_sem=rsem,
            device_id={"qa": qa, "qb": lax.rem(qb + 1, nqb)},
            device_id_type=MESH,
        ).start()
        dst[:, pl.ds(me, 1), :] = src[:, pl.ds(me, 1), :]

    def landed(dst, rsem):
        whole = dst.at[:, pl.ds(0, n), :]
        pltpu.make_async_copy(whole, whole, rsem).wait()

    turn_sin, turn_cos = sincos(turns[...])

    def pair(layer, group):
        return turn_cos[layer : layer + 1, group : group + 1], turn_sin[layer : layer + 1, group : group + 1]

    bits = n.bit_length() - 1
    low = nqb.bit_length() - 1

    def build(slot, layer, groups, left):
        real, imag = rotation(n, [pair(layer, g) for g in groups])
        if left:
            whole = jnp.concatenate(
                [jnp.concatenate([real, -imag], axis=1), jnp.concatenate([imag, real], axis=1)], axis=0
            )
        else:
            whole = jnp.concatenate(
                [jnp.concatenate([real, imag], axis=1), jnp.concatenate([-imag, real], axis=1)], axis=0
            )
        high, rest = split(whole)
        mats[slot, 0] = high
        mats[slot, 1] = rest

    device_groups = [3] * low + [2] * (bits - low)
    LANE1, ROW1, DEV1, LANE2, ROW2, DEV2, DEV3, ROW3, LANE3 = range(9)

    def mat(slot):
        return mats[slot, 0], mats[slot, 1]

    def left(slot, xr, xi):
        both = dot3(mat(slot), split(jnp.concatenate([xr, xi], axis=0)))
        return both[:n], both[n:]

    def right(slot, xr, xi):
        both = dot3(split(jnp.concatenate([xr, xi], axis=1)), mat(slot))
        return both[:, :n], both[:, n:]

    def turned(slot, xr, xi):
        both = dot3(mat(slot), split(jnp.concatenate([xr, xi], axis=1)), ((1,), (1,)))
        return both[:n], both[n:]

    for b in range(blocks):
        flip[b] = levels[b].T
    pl.semaphore_wait(bar, n - 1)
    spread(levels, tab2, tsend.at[0], trecv.at[0])

    build(LANE1, 0, [0] * bits, False)
    build(ROW1, 0, [1] * bits, True)
    parts = [phased(wave[0, b], wave[1, b], diag[0:1, :] * levels[b]) for b in range(blocks)]
    parts = mix_blocks(parts, *pair(0, 2))
    for b in range(blocks):
        work[b, 0], work[b, 1] = parts[b]

    @pl.loop(0, blocks)
    def _(b):
        xr, xi = right(LANE1, work[b, 0], work[b, 1])
        send1[b, 0], send1[b, 1] = left(ROW1, xr, xi)
        spread(send1.at[b], land1.at[b], ssem.at[b], rsem.at[b])

    build(DEV1, 0, device_groups, True)
    build(LANE2, 1, [0] * bits, True)
    build(ROW2, 1, [1] * bits, True)
    build(DEV2, 1, device_groups, True)
    build(DEV3, 2, device_groups, True)
    build(ROW3, 2, [1] * bits, False)
    build(LANE3, 2, [0] * bits, False)

    landed(tab2, trecv.at[0])

    @pl.loop(0, blocks)
    def _(b):
        landed(land1.at[b], rsem.at[b])
        xr, xi = left(DEV1, land1[b, 0, :n, :], land1[b, 1, :n, :])
        xr, xi = phased(xr, xi, diag[1:2, :] * tab2[b, :n, :])
        send2[b, 0], send2[b, 1] = turned(LANE2, xr, xi)
        spread(send2.at[b], land2.at[b], ssem.at[blocks + b], rsem.at[blocks + b])

    spread(flip, tab3, tsend.at[1], trecv.at[1])

    @pl.loop(0, blocks)
    def _(b):
        landed(land2.at[b], rsem.at[blocks + b])
        xr, xi = left(ROW2, land2[b, 0, :n, :], land2[b, 1, :n, :])
        work[b, 0], work[b, 1] = turned(DEV2, xr, xi)

    parts = mix_blocks([(work[b, 0], work[b, 1]) for b in range(blocks)], *pair(1, 2))
    for b in range(blocks):
        work[b, 0], work[b, 1] = parts[b]
    landed(tab3, trecv.at[1])
    lane = lax.broadcasted_iota(jnp.int32, (1, n), 1)
    own = jnp.sum(jnp.where(lane == me, diag[2:3, :], 0.0), axis=1, keepdims=True)

    @pl.loop(0, blocks)
    def _(b):
        xr, xi = phased(work[b, 0], work[b, 1], own * tab3[b, :n, :])
        xr, xi = left(DEV3, xr, xi)
        send3[b, 0], send3[b, 1] = right(ROW3, xr, xi)
        spread(send3.at[b], land3.at[b], ssem.at[2 * blocks + b], rsem.at[2 * blocks + b])

    @pl.loop(0, blocks)
    def _(b):
        landed(land3.at[b], rsem.at[2 * blocks + b])
        work[b, 0], work[b, 1] = right(LANE3, land3[b, 0, :n, :].T, land3[b, 1, :n, :].T)

    parts = mix_blocks([(work[b, 0], work[b, 1]) for b in range(blocks)], *pair(2, 2))
    for b in range(blocks):
        out[0, b], out[1, b] = parts[b]

    @pl.loop(0, blocks)
    def _(b):
        for k, (src, dst) in enumerate(((send1, land1), (send2, land2), (send3, land3))):
            landed(dst.at[b], ssem.at[k * blocks + b])

    landed(tab2, tsend.at[0])
    landed(tab3, tsend.at[1])


def solution(mesh):
    nqa, nqb = mesh.shape["qa"], mesh.shape["qb"]

    def shards(wave_parts, level_table, diagonal_angles, turn_angles):
        _, blocks, rows, lanes = wave_parts.shape
        state = pltpu.VMEM((blocks, 2, rows, lanes), F32)
        landing = pltpu.VMEM((blocks, 2, rows + PAD, lanes), F32)
        vmem = pl.BlockSpec(memory_space=pltpu.VMEM)
        return pl.pallas_call(
            functools.partial(body, nqa, nqb),
            out_shape=jax.ShapeDtypeStruct(wave_parts.shape, F32),
            in_specs=[vmem] * 4,
            out_specs=vmem,
            scratch_shapes=[
                pltpu.VMEM((9, 2, 2 * rows, 2 * lanes), BF16),
                state,
                state,
                state,
                landing,
                landing,
                landing,
                pltpu.VMEM((blocks, rows, lanes), F32),
                pltpu.VMEM((blocks, rows + PAD, lanes), F32),
                pltpu.VMEM((blocks, rows + PAD, lanes), F32),
                state,
                pltpu.SemaphoreType.DMA((3 * blocks,)),
                pltpu.SemaphoreType.DMA((3 * blocks,)),
                pltpu.SemaphoreType.DMA((2,)),
                pltpu.SemaphoreType.DMA((2,)),
            ],
            name="layers",
            compiler_params=pltpu.CompilerParams(collective_id=0, has_side_effects=True),
        )(wave_parts, level_table, diagonal_angles, turn_angles)

    return jax.shard_map(
        shards,
        mesh=mesh,
        in_specs=(
            P("trial", ("qa", "qb"), None, None),
            P(("trial", "qa", "qb"), None, None),
            P("trial", None),
            P("trial", None),
        ),
        out_specs=P("trial", ("qa", "qb"), None, None),
        check_vma=False,
    )
```

time: 246 us -> 81.3 us (0.33)
  waiting for transfers between devices: 87 us -> 0 us
  Pallas kernels: 0 us -> 78.9 us
  blocking collectives: 54.3 us -> 0 us
  starting transfers between devices: 43.6 us -> 0 us
  matrix products: 20.9 us -> 0 us
  between operations: 17.6 us -> 0.01 us
  local copies, waits for them, and re-layouts: 15.4 us -> 1.87 us
  other arithmetic: 5.26 us -> 0 us
    all_to_all x8 -> x0, waiting for transfers between devices: 87 us -> none  [the longest x3 40.4 us: shards(): lax.all_to_all(values, 'qb', split_axis=3, concat_axis=1, tiled=True)]
    pallas_call x0 -> x1, Pallas kernels: none -> 78.9 us  [shards(): pl.pallas_call(functools.partial(body, nqa, nqb), out_shape=jax.ShapeDtyp...]
    all_to_all x4 -> x0, blocking collectives: 54.3 us -> none  [the longest x3 39 us: shards(): lax.all_to_all(moved, 'qa', split_axis=1, concat_axis=2, tiled=True)]
    all_to_all x8 -> x0, starting transfers between devices: 43.6 us -> none  [the longest x3 20.8 us: shards(): lax.all_to_all(values, 'qa', split_axis=2, concat_axis=1, tiled=True)]
    dot_general x24 -> x0, matrix products: 20.9 us -> none  [times(): jnp.tensordot(values, table, axes=([dim], [0]), precision=lax.Precision.H...]
    another operation x9 -> x0, local copies, waits for them, and re-layouts: 5.69 us -> none  [mix_dim(): return jnp.stack([by_real[0] - by_imag[1], by_real[1] + by_imag[0]])]
    all_to_all x16 -> x0, local copies, waits for them, and re-layouts: 5.52 us -> none  [the longest x6 3.09 us: shards(): lax.all_to_all(moved, 'qa', split_axis=1, concat_axis=2, tiled=True)]
    another operation x12 -> x0, other arithmetic: 4.42 us -> none  [the longest x3 4.08 us: phase_step(): jnp.stack([values[0] * jnp.cos(turn) + values[1] * jnp.sin(turn), values[...]
  transfers between devices with their start and end apart: 8 -> 0, of which waited for: 8 -> 0; matrix products, arithmetic and copies ran while one was open for 0% -> 0% of each run, Pallas kernels for 0% -> 0%
where the time goes in v1:
time: 81.3 us; the launch traced here: 80.8 us
  Pallas kernels  78.9 us (97%)
  local copies, waits for them, and re-layouts  1.87 us (2%)
    pallas_call x1, Pallas kernels, shards(): pl.pallas_call(functools.partial(body, nqa, nqb), out_shape=jax.ShapeDtyp...  78.9 us
    unnamed x1, local copies, waits for them, and re-layouts  1.87 us

profile of v1, /device:TPU:2, one launch (start us, length us, event | category | flops | bytes accessed | tf_op | source)
XLA Modules:
  0.0 80.8 jit_solution(2457270698385176464)
XLA Ops:
  0.0 78.9 %layers.1 = f32[2,4,128,128]{3,2,1,0:T(8,128)} custom-call(f32[2,4,128,128]{3,2,1,0:T(8,128)} %wave.1, f32[4,128,128]{2,1,0:T(8,128)} %levels.1, f32[3,128]{1,0:T(4,128)} %diag.1, f32[3,4]{1,0:T(4,128)} %turns.1), custom_call_target="tpu_custom_call" | custom-call | tf_op jit(solution)/shard_map/layers/pallas_call | solution.py:272
  78.9 1.9 %copy.6 = f32[2,4,128,128]{3,2,1,0:T(8,128)} copy(f32[2,4,128,128]{3,2,1,0:T(8,128)} %layers.1) | data formatting | bytes 1048576

commit v2 on v1

--- a/solution.py
+++ b/solution.py
@@ -11,6 +11,8 @@
 F32 = jnp.float32
 BF16 = jnp.bfloat16
 PAD = 8
+GROUP = 4
+EARLY = True
 
 
 def split(x):
@@ -122,8 +124,8 @@
     def spread(src, dst, ssem, rsem):
         def visit(a, z):
             pltpu.make_async_remote_copy(
-                src_ref=src.at[:, pl.ds(a * nqb + z, 1), :],
-                dst_ref=dst.at[:, pl.ds(me, 1), :],
+                src_ref=src.at[..., pl.ds(a * nqb + z, 1), :],
+                dst_ref=dst.at[..., pl.ds(me, 1), :],
                 send_sem=ssem,
                 recv_sem=rsem,
                 device_id={"qa": a, "qb": z},
@@ -132,17 +134,24 @@
 
         peers(visit)
         pltpu.make_async_remote_copy(
-            src_ref=src.at[:, pl.ds(0, 1), :],
-            dst_ref=dst.at[:, pl.ds(n, 1), :],
+            src_ref=src.at[..., pl.ds(0, 1), :],
+            dst_ref=dst.at[..., pl.ds(n, 1), :],
             send_sem=ssem,
             recv_sem=rsem,
             device_id={"qa": qa, "qb": lax.rem(qb + 1, nqb)},
             device_id_type=MESH,
         ).start()
-        dst[:, pl.ds(me, 1), :] = src[:, pl.ds(me, 1), :]
+        dst[..., pl.ds(me, 1), :] = src[..., pl.ds(me, 1), :]
+
+    def swap(k, i):
+        part = pl.ds(i * GROUP, GROUP)
+        spread((send1, send2, send3)[k].at[part], (land1, land2, land3)[k].at[part], ssem.at[k, i], rsem.at[k, i])
+
+    def arrived(k, i, sems):
+        landed((land1, land2, land3)[k].at[pl.ds(i * GROUP, GROUP)], sems.at[k, i])
 
     def landed(dst, rsem):
-        whole = dst.at[:, pl.ds(0, n), :]
+        whole = dst.at[..., pl.ds(0, n), :]
         pltpu.make_async_copy(whole, whole, rsem).wait()
 
     turn_sin, turn_cos = sincos(turns[...])
@@ -197,11 +206,17 @@
     for b in range(blocks):
         work[b, 0], work[b, 1] = parts[b]
 
-    @pl.loop(0, blocks)
-    def _(b):
-        xr, xi = right(LANE1, work[b, 0], work[b, 1])
-        send1[b, 0], send1[b, 1] = left(ROW1, xr, xi)
-        spread(send1.at[b], land1.at[b], ssem.at[b], rsem.at[b])
+    @pl.loop(0, blocks // GROUP)
+    def _(i):
+        @pl.loop(i * GROUP, i * GROUP + GROUP)
+        def _(b):
+            xr, xi = right(LANE1, work[b, 0], work[b, 1])
+            send1[b, 0], send1[b, 1] = left(ROW1, xr, xi)
+
+        swap(0, i)
+
+    if EARLY:
+        spread(flip, tab3, tsend.at[1], trecv.at[1])
 
     build(DEV1, 0, device_groups, True)
     build(LANE2, 1, [0] * bits, True)
@@ -213,21 +228,29 @@
 
     landed(tab2, trecv.at[0])
 
-    @pl.loop(0, blocks)
-    def _(b):
-        landed(land1.at[b], rsem.at[b])
-        xr, xi = left(DEV1, land1[b, 0, :n, :], land1[b, 1, :n, :])
-        xr, xi = phased(xr, xi, diag[1:2, :] * tab2[b, :n, :])
-        send2[b, 0], send2[b, 1] = turned(LANE2, xr, xi)
-        spread(send2.at[b], land2.at[b], ssem.at[blocks + b], rsem.at[blocks + b])
-
-    spread(flip, tab3, tsend.at[1], trecv.at[1])
-
-    @pl.loop(0, blocks)
-    def _(b):
-        landed(land2.at[b], rsem.at[blocks + b])
-        xr, xi = left(ROW2, land2[b, 0, :n, :], land2[b, 1, :n, :])
-        work[b, 0], work[b, 1] = turned(DEV2, xr, xi)
+    @pl.loop(0, blocks // GROUP)
+    def _(i):
+        arrived(0, i, rsem)
+
+        @pl.loop(i * GROUP, i * GROUP + GROUP)
+        def _(b):
+            xr, xi = left(DEV1, land1[b, 0, :n, :], land1[b, 1, :n, :])
+            xr, xi = phased(xr, xi, diag[1:2, :] * tab2[b, :n, :])
+            send2[b, 0], send2[b, 1] = turned(LANE2, xr, xi)
+
+        swap(1, i)
+
+    if not EARLY:
+        spread(flip, tab3, tsend.at[1], trecv.at[1])
+
+    @pl.loop(0, blocks // GROUP)
+    def _(i):
+        arrived(1, i, rsem)
+
+        @pl.loop(i * GROUP, i * GROUP + GROUP)
+        def _(b):
+            xr, xi = left(ROW2, land2[b, 0, :n, :], land2[b, 1, :n, :])
+            work[b, 0], work[b, 1] = turned(DEV2, xr, xi)
 
     parts = mix_blocks([(work[b, 0], work[b, 1]) for b in range(blocks)], *pair(1, 2))
     for b in range(blocks):
@@ -236,26 +259,32 @@
     lane = lax.broadcasted_iota(jnp.int32, (1, n), 1)
     own = jnp.sum(jnp.where(lane == me, diag[2:3, :], 0.0), axis=1, keepdims=True)
 
-    @pl.loop(0, blocks)
-    def _(b):
-        xr, xi = phased(work[b, 0], work[b, 1], own * tab3[b, :n, :])
-        xr, xi = left(DEV3, xr, xi)
-        send3[b, 0], send3[b, 1] = right(ROW3, xr, xi)
-        spread(send3.at[b], land3.at[b], ssem.at[2 * blocks + b], rsem.at[2 * blocks + b])
-
-    @pl.loop(0, blocks)
-    def _(b):
-        landed(land3.at[b], rsem.at[2 * blocks + b])
-        work[b, 0], work[b, 1] = right(LANE3, land3[b, 0, :n, :].T, land3[b, 1, :n, :].T)
+    @pl.loop(0, blocks // GROUP)
+    def _(i):
+        @pl.loop(i * GROUP, i * GROUP + GROUP)
+        def _(b):
+            xr, xi = phased(work[b, 0], work[b, 1], own * tab3[b, :n, :])
+            xr, xi = left(DEV3, xr, xi)
+            send3[b, 0], send3[b, 1] = right(ROW3, xr, xi)
+
+        swap(2, i)
+
+    @pl.loop(0, blocks // GROUP)
+    def _(i):
+        arrived(2, i, rsem)
+
+        @pl.loop(i * GROUP, i * GROUP + GROUP)
+        def _(b):
+            work[b, 0], work[b, 1] = right(LANE3, land3[b, 0, :n, :].T, land3[b, 1, :n, :].T)
 
     parts = mix_blocks([(work[b, 0], work[b, 1]) for b in range(blocks)], *pair(2, 2))
     for b in range(blocks):
         out[0, b], out[1, b] = parts[b]
 
-    @pl.loop(0, blocks)
-    def _(b):
-        for k, (src, dst) in enumerate(((send1, land1), (send2, land2), (send3, land3))):
-            landed(dst.at[b], ssem.at[k * blocks + b])
+    @pl.loop(0, blocks // GROUP)
+    def _(i):
+        for k in range(3):
+            arrived(k, i, ssem)
 
     landed(tab2, tsend.at[0])
     landed(tab3, tsend.at[1])
@@ -286,8 +315,8 @@
                 pltpu.VMEM((blocks, rows + PAD, lanes), F32),
                 pltpu.VMEM((blocks, rows + PAD, lanes), F32),
                 state,
-                pltpu.SemaphoreType.DMA((3 * blocks,)),
-                pltpu.SemaphoreType.DMA((3 * blocks,)),
+                pltpu.SemaphoreType.DMA((3, blocks // GROUP)),
+                pltpu.SemaphoreType.DMA((3, blocks // GROUP)),
                 pltpu.SemaphoreType.DMA((2,)),
                 pltpu.SemaphoreType.DMA((2,)),
             ],

time: 81.3 us -> 73.4 us (0.903)
  Pallas kernels: 78.9 us -> 71.4 us
    pallas_call x1, Pallas kernels: 78.9 us -> 71.4 us  [shards(): pl.pallas_call(functools.partial(body, nqa, nqb), out_shape=jax.ShapeDtyp...]
where the time goes in v2:
time: 73.4 us; the launch traced here: 73.3 us
  Pallas kernels  71.4 us (97%)
  local copies, waits for them, and re-layouts  1.87 us (3%)
    pallas_call x1, Pallas kernels, shards(): pl.pallas_call(functools.partial(body, nqa, nqb), out_shape=jax.ShapeDtyp...  71.4 us
    unnamed x1, local copies, waits for them, and re-layouts  1.87 us

profile of v2, /device:TPU:2, one launch (start us, length us, event | category | flops | bytes accessed | tf_op | source)
XLA Modules:
  0.0 73.3 jit_solution(11381196780820888700)
XLA Ops:
  0.0 71.4 %layers.1 = f32[2,4,128,128]{3,2,1,0:T(8,128)} custom-call(f32[2,4,128,128]{3,2,1,0:T(8,128)} %wave.1, f32[4,128,128]{2,1,0:T(8,128)} %levels.1, f32[3,128]{1,0:T(4,128)} %diag.1, f32[3,4]{1,0:T(4,128)} %turns.1), custom_call_target="tpu_custom_call" | custom-call | tf_op jit(solution)/shard_map/layers/pallas_call | solution.py:301
  71.4 1.9 %copy.6 = f32[2,4,128,128]{3,2,1,0:T(8,128)} copy(f32[2,4,128,128]{3,2,1,0:T(8,128)} %layers.1) | data formatting | bytes 1048576

commit v3 on v1

--- a/solution.py
+++ b/solution.py
@@ -41,9 +41,12 @@
     return sin, cos
 
 
+def rotated(xr, xi, s, c):
+    return xr * c + xi * s, xi * c - xr * s
+
+
 def phased(xr, xi, turn):
-    s, c = sincos(turn)
-    return xr * c + xi * s, xi * c - xr * s
+    return rotated(xr, xi, *sincos(turn))
 
 
 def rotation(count, pairs):
@@ -94,6 +97,7 @@
     tab2,
     tab3,
     work,
+    phase,
     ssem,
     rsem,
     tsend,
@@ -122,8 +126,8 @@
     def spread(src, dst, ssem, rsem):
         def visit(a, z):
             pltpu.make_async_remote_copy(
-                src_ref=src.at[:, pl.ds(a * nqb + z, 1), :],
-                dst_ref=dst.at[:, pl.ds(me, 1), :],
+                src_ref=src.at[..., pl.ds(a * nqb + z, 1), :],
+                dst_ref=dst.at[..., pl.ds(me, 1), :],
                 send_sem=ssem,
                 recv_sem=rsem,
                 device_id={"qa": a, "qb": z},
@@ -132,17 +136,23 @@
 
         peers(visit)
         pltpu.make_async_remote_copy(
-            src_ref=src.at[:, pl.ds(0, 1), :],
-            dst_ref=dst.at[:, pl.ds(n, 1), :],
+            src_ref=src.at[..., pl.ds(0, 1), :],
+            dst_ref=dst.at[..., pl.ds(n, 1), :],
             send_sem=ssem,
             recv_sem=rsem,
             device_id={"qa": qa, "qb": lax.rem(qb + 1, nqb)},
             device_id_type=MESH,
         ).start()
-        dst[:, pl.ds(me, 1), :] = src[:, pl.ds(me, 1), :]
+        dst[..., pl.ds(me, 1), :] = src[..., pl.ds(me, 1), :]
+
+    def swap(k):
+        spread((send1, send2, send3)[k], (land1, land2, land3)[k], ssem.at[k], rsem.at[k])
+
+    def arrived(k, sems):
+        landed((land1, land2, land3)[k], sems.at[k])
 
     def landed(dst, rsem):
-        whole = dst.at[:, pl.ds(0, n), :]
+        whole = dst.at[..., pl.ds(0, n), :]
         pltpu.make_async_copy(whole, whole, rsem).wait()
 
     turn_sin, turn_cos = sincos(turns[...])
@@ -187,21 +197,20 @@
 
     for b in range(blocks):
         flip[b] = levels[b].T
-    pl.semaphore_wait(bar, n - 1)
-    spread(levels, tab2, tsend.at[0], trecv.at[0])
-
     build(LANE1, 0, [0] * bits, False)
     build(ROW1, 0, [1] * bits, True)
     parts = [phased(wave[0, b], wave[1, b], diag[0:1, :] * levels[b]) for b in range(blocks)]
     parts = mix_blocks(parts, *pair(0, 2))
     for b in range(blocks):
         work[b, 0], work[b, 1] = parts[b]
-
-    @pl.loop(0, blocks)
-    def _(b):
+    pl.semaphore_wait(bar, n - 1)
+    spread(levels, tab2, tsend.at[0], trecv.at[0])
+    for b in range(blocks):
         xr, xi = right(LANE1, work[b, 0], work[b, 1])
         send1[b, 0], send1[b, 1] = left(ROW1, xr, xi)
-        spread(send1.at[b], land1.at[b], ssem.at[b], rsem.at[b])
+    swap(0)
+
+    spread(flip, tab3, tsend.at[1], trecv.at[1])
 
     build(DEV1, 0, device_groups, True)
     build(LANE2, 1, [0] * bits, True)
@@ -212,50 +221,41 @@
     build(LANE3, 2, [0] * bits, False)
 
     landed(tab2, trecv.at[0])
-
-    @pl.loop(0, blocks)
-    def _(b):
-        landed(land1.at[b], rsem.at[b])
+    for b in range(blocks):
+        phase[b, 0], phase[b, 1] = sincos(diag[1:2, :] * tab2[b, :n, :])
+    arrived(0, rsem)
+    for b in range(blocks):
         xr, xi = left(DEV1, land1[b, 0, :n, :], land1[b, 1, :n, :])
-        xr, xi = phased(xr, xi, diag[1:2, :] * tab2[b, :n, :])
+        xr, xi = rotated(xr, xi, phase[b, 0], phase[b, 1])
         send2[b, 0], send2[b, 1] = turned(LANE2, xr, xi)
-        spread(send2.at[b], land2.at[b], ssem.at[blocks + b], rsem.at[blocks + b])
-
-    spread(flip, tab3, tsend.at[1], trecv.at[1])
-
-    @pl.loop(0, blocks)
-    def _(b):
-        landed(land2.at[b], rsem.at[blocks + b])
+    swap(1)
+
+    lane = lax.broadcasted_iota(jnp.int32, (1, n), 1)
+    own = jnp.sum(jnp.where(lane == me, diag[2:3, :], 0.0), axis=1, keepdims=True)
+    landed(tab3, trecv.at[1])
+    for b in range(blocks):
+        phase[b, 0], phase[b, 1] = sincos(own * tab3[b, :n, :])
+    arrived(1, rsem)
+    for b in range(blocks):
         xr, xi = left(ROW2, land2[b, 0, :n, :], land2[b, 1, :n, :])
         work[b, 0], work[b, 1] = turned(DEV2, xr, xi)
-
     parts = mix_blocks([(work[b, 0], work[b, 1]) for b in range(blocks)], *pair(1, 2))
     for b in range(blocks):
-        work[b, 0], work[b, 1] = parts[b]
-    landed(tab3, trecv.at[1])
-    lane = lax.broadcasted_iota(jnp.int32, (1, n), 1)
-    own = jnp.sum(jnp.where(lane == me, diag[2:3, :], 0.0), axis=1, keepdims=True)
-
-    @pl.loop(0, blocks)
-    def _(b):
-        xr, xi = phased(work[b, 0], work[b, 1], own * tab3[b, :n, :])
-        xr, xi = left(DEV3, xr, xi)
-        send3[b, 0], send3[b, 1] = right(ROW3, xr, xi)
-        spread(send3.at[b], land3.at[b], ssem.at[2 * blocks + b], rsem.at[2 * blocks + b])
-
-    @pl.loop(0, blocks)
-    def _(b):
-        landed(land3.at[b], rsem.at[2 * blocks + b])
+        xr, xi = rotated(*parts[b], phase[b, 0], phase[b, 1])
+        work[b, 0], work[b, 1] = left(DEV3, xr, xi)
+    for b in range(blocks):
+        send3[b, 0], send3[b, 1] = right(ROW3, work[b, 0], work[b, 1])
+    swap(2)
+
+    arrived(2, rsem)
+    for b in range(blocks):
         work[b, 0], work[b, 1] = right(LANE3, land3[b, 0, :n, :].T, land3[b, 1, :n, :].T)
-
     parts = mix_blocks([(work[b, 0], work[b, 1]) for b in range(blocks)], *pair(2, 2))
     for b in range(blocks):
         out[0, b], out[1, b] = parts[b]
 
-    @pl.loop(0, blocks)
-    def _(b):
-        for k, (src, dst) in enumerate(((send1, land1), (send2, land2), (send3, land3))):
-            landed(dst.at[b], ssem.at[k * blocks + b])
+    for k in range(3):
+        arrived(k, ssem)
 
     landed(tab2, tsend.at[0])
     landed(tab3, tsend.at[1])
@@ -286,8 +286,9 @@
                 pltpu.VMEM((blocks, rows + PAD, lanes), F32),
                 pltpu.VMEM((blocks, rows + PAD, lanes), F32),
                 state,
-                pltpu.SemaphoreType.DMA((3 * blocks,)),
-                pltpu.SemaphoreType.DMA((3 * blocks,)),
+                state,
+                pltpu.SemaphoreType.DMA((3,)),
+                pltpu.SemaphoreType.DMA((3,)),
                 pltpu.SemaphoreType.DMA((2,)),
                 pltpu.SemaphoreType.DMA((2,)),
             ],

time: 81.3 us -> 70.1 us (0.86)
  Pallas kernels: 78.9 us -> 68.1 us
    pallas_call x1, Pallas kernels: 78.9 us -> 68.1 us  [shards(): pl.pallas_call(functools.partial(body, nqa, nqb), out_shape=jax.ShapeDtyp...]
where the time goes in v3:
time: 70.1 us; the launch traced here: 70 us
  Pallas kernels  68.1 us (97%)
  local copies, waits for them, and re-layouts  1.87 us (3%)
    pallas_call x1, Pallas kernels, shards(): pl.pallas_call(functools.partial(body, nqa, nqb), out_shape=jax.ShapeDtyp...  68.1 us
    unnamed x1, local copies, waits for them, and re-layouts  1.87 us

profile of v3, /device:TPU:2, one launch (start us, length us, event | category | flops | bytes accessed | tf_op | source)
XLA Modules:
  0.0 70.0 jit_solution(9312278608322851936)
XLA Ops:
  0.0 68.1 %layers.1 = f32[2,4,128,128]{3,2,1,0:T(8,128)} custom-call(f32[2,4,128,128]{3,2,1,0:T(8,128)} %wave.1, f32[4,128,128]{2,1,0:T(8,128)} %levels.1, f32[3,128]{1,0:T(4,128)} %diag.1, f32[3,4]{1,0:T(4,128)} %turns.1), custom_call_target="tpu_custom_call" | custom-call | tf_op jit(solution)/shard_map/layers/pallas_call | solution.py:272
  68.1 1.9 %copy.6 = f32[2,4,128,128]{3,2,1,0:T(8,128)} copy(f32[2,4,128,128]{3,2,1,0:T(8,128)} %layers.1) | data formatting | bytes 1048576
